TPU v7x, 16 devices: a 4x2x1 block of a 4x4x8 slice. The times are simulated.
16 devices in a mesh: dp: 2 (over y, z), ws: 8 (over x, core).
Axes of the slice: x: 4, y: 2, z: 1, core: 2. Of those that a mesh axis runs over, the one named last changes fastest.
The devices are a block of a 4x4x8 slice.
Arguments:
- hidden: bfloat16 [256, 768], P(('dp', 'ws')), parts along dimension 0
- self_k: bfloat16 [256, 12, 384, 64], P(('dp', 'ws')), parts along dimension 0
- self_v: bfloat16 [256, 12, 384, 64], P(('dp', 'ws')), parts along dimension 0
- cross_k: bfloat16 [256, 12, 1024, 64], P(('dp', 'ws')), parts along dimension 0
- cross_v: bfloat16 [256, 12, 1024, 64], P(('dp', 'ws')), parts along dimension 0
- positions: int32 [256], P(('dp', 'ws')), parts along dimension 0
- enc_mask: int32 [256, 1024], P(('dp', 'ws')), parts along dimension 0
- rel_bias: float32 [12, 384], replicated
- expert_idx: int32 [256], P(('dp', 'ws')), parts along dimension 0
- ln_self: float32 [768], replicated
- ln_cross: float32 [768], replicated
- ln_ffn: float32 [768], replicated
- wq_self: bfloat16 [768, 768], P(None, 'ws')
- wk_self: bfloat16 [768, 768], P(None, 'ws')
- wv_self: bfloat16 [768, 768], P(None, 'ws')
- wo_self: bfloat16 [768, 768], P(None, 'ws')
- wq_cross: bfloat16 [768, 768], P(None, 'ws')
- wo_cross: bfloat16 [768, 768], P(None, 'ws')
- w_router: float32 [768, 8], P(None, 'ws')
- w_in: bfloat16 [8, 768, 3072], P(None, None, 'ws')
- w_out: bfloat16 [8, 3072, 768], P(None, 'ws')
Outputs:
- output 1: bfloat16 [256, 768], P(('dp', 'ws')), parts along dimension 0
- output 2: bfloat16 [256, 12, 384, 64], P(('dp', 'ws')), parts along dimension 0
- output 3: bfloat16 [256, 12, 384, 64], P(('dp', 'ws')), parts along dimension 0
There are 2 independent parts. A program takes and returns all parts, laid end to end along the dimension named above; an argument that names none is the same for every part.
All inputs are finite; a program needn't handle non-finite values.
Results may differ from a plain program's by a relative error of at most 0.0110425.
Values are sent between devices in bfloat16 or wider.
A program may use at most 768 MiB of HBM per device.

v0:
```python
import functools
import jax
import jax.numpy as jnp
from jax import lax
from jax.experimental import pallas as pl
from jax.experimental.pallas import tpu as pltpu
from jax.sharding import PartitionSpec as P

EPSILON = 1e-6
NEG_BIG = -1e30
MESH = pl.DeviceIdType.MESH
F32 = jnp.float32
BF16 = jnp.bfloat16
CHUNK = 256
GROUP = 4
SLOTS = 24
SELF_VMEM = 16 * 1024 * 1024
CROSS_VMEM = 18 * 1024 * 1024
FFN_VMEM = 20 * 1024 * 1024

vmem = functools.partial(pl.BlockSpec, memory_space=pltpu.VMEM)
smem = functools.partial(pl.BlockSpec, memory_space=pltpu.SMEM)
hbm = functools.partial(pl.BlockSpec, memory_space=pltpu.HBM)


def rms(hid_f32, scale):
    inv = lax.rsqrt(jnp.mean(hid_f32 * hid_f32, axis=-1, keepdims=True) + EPSILON)
    return (hid_f32 * inv * scale.reshape(1, -1)).astype(BF16)


def dot_nn(a, b):
    return lax.dot_general(a, b, (((1,), (0,)), ((), ())), preferred_element_type=F32)


def dot_nt(a, b):
    return lax.dot_general(a, b, (((1,), (1,)), ((), ())), preferred_element_type=F32)


def remote(src, dst, send, recv, dev):
    return pltpu.make_async_remote_copy(src_ref=src, dst_ref=dst, send_sem=send, recv_sem=recv,
                                        device_id={"ws": dev}, device_id_type=MESH)


def enter(me, n):
    barrier = pltpu.get_barrier_semaphore()
    for d in range(1, n):
        pl.semaphore_signal(barrier, inc=1, device_id={"ws": lax.rem(me + d, n)}, device_id_type=MESH)
    pl.semaphore_wait(barrier, n - 1)


def rows_of(ref, i, rows):
    return ref.at[pl.ds(pl.multiple_of(i * rows, rows), rows)]


def head_mask(heads_pad, width, head_dim):
    sub = lax.broadcasted_iota(jnp.int32, (heads_pad, width), 0) * head_dim
    lane = lax.broadcasted_iota(jnp.int32, (heads_pad, width), 1)
    return (lane >= sub) & (lane < sub + head_dim)


def softmax_rows(s):
    e = jnp.exp(s - jnp.max(s, axis=-1, keepdims=True))
    return e * (1.0 / jnp.sum(e, axis=-1, keepdims=True))


def self_kernel(n, heads, pos_ref, hid_ref, mask_ref, relb_ref, ln1_ref, ln2_ref, wq_ref, wk_ref, wv_ref,
                wo_ref, wqc_ref, woc_ref, sk_ref, sv_ref, ck_ref, cv_ref,
                qc_out, h1_out, lens_out, woc_out, kbuf, vbuf, khead, vhead,
                hall, stage, got, wqkv, wall, q_s, k_s, v_s, kt_s, vt_s, qbd, snew, ctx_s, relrev,
                lsem, ksem, vsem, chsem, hsend, hrecv, asend, arecv, wsend, wrecv, fsend, frecv, lsend, lrecv):
    me = lax.axis_index("ws")
    rows, model = hid_ref.shape
    cols = wq_ref.shape[0]
    width = cols * n
    cache_len = sk_ref.shape[2]
    heads_pad = qbd.shape[0] // rows
    head_dim = width // heads
    chips = n // 2

    locals_ = [pltpu.make_async_copy(w, wqkv.at[i], lsem.at[i]) for i, w in enumerate((wq_ref, wk_ref, wv_ref))]
    locals_ += [pltpu.make_async_copy(w, rows_of(wall.at[i], me, cols), lsem.at[3 + i])
                for i, w in enumerate((wo_ref, wqc_ref, woc_ref))]
    for copy in locals_:
        copy.start()
    for b in range(rows):
        pltpu.make_async_copy(sk_ref.at[b], kbuf.at[b], ksem.at[b]).start()
        pltpu.make_async_copy(sv_ref.at[b], vbuf.at[b], vsem.at[b]).start()
    heads_of = [pltpu.make_async_copy(src.at[:, :, pl.ds(0, CHUNK)], dst, chsem.at[i])
                for i, (src, dst) in enumerate(((ck_ref, khead), (cv_ref, vhead)))]
    for copy in heads_of:
        copy.start()

    stage[...] = jnp.zeros_like(stage)
    enter(me, n)

    def h_copy(src, dev):
        return remote(hid_ref, rows_of(hall, src, rows), hsend.at[dev], hrecv.at[src], dev)

    for d in range(1, n):
        h_copy(me, lax.rem(me + d, n)).start()

    chip, core = me // 2, lax.rem(me, 2)
    def w_copy(t, src, dev):
        piece = rows_of(wall.at[t], src, cols)
        return remote(piece, piece, wsend.at[t, dev], wrecv.at[t, src], dev)

    def f_copy(t, src, dev):
        piece = rows_of(wall.at[t], src, cols)
        return remote(piece, piece, fsend.at[t, src], frecv.at[t, src], dev)

    def across(d):
        return lax.rem(chip + d, chips) * 2 + core

    half = cols // 2
    right, left, far, partner = across(1), across(3), across(2), me + 1 - 2 * core

    def l_copy(t, side, src, dev):
        piece = wall.at[t].at[pl.ds(pl.multiple_of(src * cols + side * half, half), half)]
        return remote(piece, piece, lsend.at[t, side], lrecv.at[t, side], dev)

    def w_start(t):
        for dev in (right, left, partner):
            w_copy(t, me, dev).start()

    def w_relay(t):
        w_copy(t, left, me).wait_recv()
        l_copy(t, 0, left, right).start()
        f_copy(t, left, partner).start()
        w_copy(t, right, me).wait_recv()
        l_copy(t, 1, right, left).start()
        f_copy(t, right, partner).start()

    def w_forward(t):
        for side in range(2):
            l_copy(t, side, far, me).wait_recv()
        f_copy(t, far, partner).start()

    def w_finish(t):
        w_copy(t, partner, me).wait_recv()
        for d in range(1, chips):
            f_copy(t, across(d) + 1 - 2 * core, me).wait_recv()

    for copy in locals_:
        copy.wait()
    w_start(0)
    hall[pl.ds(pl.multiple_of(me * rows, rows), rows), :] = hid_ref[...]

    rb = relb_ref[...]
    rev = (lax.broadcasted_iota(jnp.int32, (cache_len, cache_len), 0)
           + lax.broadcasted_iota(jnp.int32, (cache_len, cache_len), 1) == cache_len - 1).astype(BF16)
    hi = rb.astype(BF16)
    mid = (rb - hi.astype(F32)).astype(BF16)
    low = (rb - hi.astype(F32) - mid.astype(F32)).astype(BF16)
    relrev[...] = jnp.zeros_like(relrev)
    relrev[0:heads, :] = dot_nn(hi, rev) + dot_nn(mid, rev) + dot_nn(low, rev)
    lens_out[...] = jnp.broadcast_to(
        jnp.sum(mask_ref[...].astype(F32), axis=-1, keepdims=True), lens_out.shape).astype(jnp.int32)

    for d in range(1, n):
        h_copy(lax.rem(me + n - d, n), me).wait_recv()
    x = rms(hall[...].astype(F32), ln1_ref[...])
    for i in range(3):
        y = dot_nt(x, wqkv[i]).astype(BF16)
        for j in range(n):
            stage[j, :, i * 128:i * 128 + cols] = y[j * rows:(j + 1) * rows, :]

    def a_copy(src, dev):
        return remote(stage.at[dev], got.at[src], asend.at[dev], arecv.at[src], dev)

    for d in range(1, n):
        a_copy(me, lax.rem(me + d, n)).start()
    got[me] = stage[me]
    w_start(1)
    w_start(2)
    for d in range(1, n):
        a_copy(lax.rem(me + n - d, n), me).wait_recv()

    lane = lax.broadcasted_iota(jnp.int32, (rows, 128), 1)
    for i, dst in enumerate((q_s, k_s, v_s)):
        tiles = [None] * (width // 128)
        for s in range(n):
            piece = got[s, :, i * 128:(i + 1) * 128].astype(F32)
            t, r = divmod(s * cols, 128)
            if r:
                piece = pltpu.roll(piece, r, axis=1)
            ends = ((t, r, min(128, r + cols)), (t + 1, 0, r + cols - 128))
            for tile, lo, hi_ in ends:
                if hi_ > lo:
                    base = jnp.zeros((rows, 128), F32) if tiles[tile] is None else tiles[tile]
                    tiles[tile] = jnp.where((lane >= lo) & (lane < hi_), piece, base)
        for t, tile in enumerate(tiles):
            dst[:, t * 128:(t + 1) * 128] = tile
    diag = head_mask(heads_pad, width, head_dim)
    for b in range(rows):
        qbd[b * heads_pad:(b + 1) * heads_pad, :] = jnp.where(
            diag, jnp.broadcast_to(q_s[b:b + 1, :], diag.shape), 0.0).astype(BF16)
    cross = dot_nt(qbd[...], k_s[...].astype(BF16))
    own = (lax.broadcasted_iota(jnp.int32, cross.shape, 0) // heads_pad
           == lax.broadcasted_iota(jnp.int32, cross.shape, 1))
    snew[...] = jnp.broadcast_to(jnp.sum(jnp.where(own, cross, 0.0), axis=-1, keepdims=True), snew.shape)
    for src, dst in ((k_s, kt_s), (v_s, vt_s)):
        flipped = jnp.transpose(src[...])
        for i in range(rows // 4):
            dst[i] = flipped[:, i * 4:(i + 1) * 4]

    col = lax.broadcasted_iota(jnp.int32, (heads_pad, cache_len), 1)
    lane16 = lax.broadcasted_iota(jnp.int32, (16, cache_len), 1)

    def insert(buf, b, here, new):
        wide = jnp.broadcast_to(new, (width, 128)).astype(BF16).reshape(width // 16, 16, 128)
        for t in range(cache_len // 128):
            part = slice(t * 128, (t + 1) * 128)
            old = buf[b, :, part].reshape(width // 16, 16, 128)
            buf[b, :, part] = jnp.where(here[None, :, part], wide, old).reshape(width, 128)

    w_relay(0)

    def quad(i, carry):
        rows4 = [i * 4 + r for r in range(4)]
        head_rows = [pl.ds(pl.multiple_of(b * heads_pad, heads_pad), heads_pad) for b in rows4]
        for b in rows4:
            pltpu.make_async_copy(sk_ref.at[b], kbuf.at[b], ksem.at[b]).wait()
            pltpu.make_async_copy(sv_ref.at[b], vbuf.at[b], vsem.at[b]).wait()
        raw = [dot_nn(qbd[hr, :], kbuf[b]) for b, hr in zip(rows4, head_rows)]
        olds, news = [], []
        for s, b, hr in zip(raw, rows4, head_rows):
            pos = pos_ref[b]
            s = jnp.where(col == pos, snew[hr, 0:1], s)
            bias = pltpu.roll(relrev[...], lax.rem(pos + 1, cache_len), axis=1)
            p = softmax_rows(jnp.where(col <= pos, s + bias, NEG_BIG)).astype(BF16).astype(F32)
            news.append(jnp.sum(jnp.where(col == pos, p, 0.0), axis=-1, keepdims=True))
            olds.append(jnp.where(col == pos, 0.0, p).astype(BF16))
        outs = [dot_nt(p, vbuf[b]) for p, b in zip(olds, rows4)]
        for c, pnew, b in zip(outs, news, rows4):
            c = c + pnew * v_s[pl.ds(b, 1), :]
            ctx_s[pl.ds(b, 1), :] = jnp.sum(jnp.where(diag, c, 0.0), axis=0, keepdims=True)
        for r, b in enumerate(rows4):
            here = lane16 == pos_ref[b]
            insert(kbuf, b, here, kt_s[i, :, r:r + 1])
            insert(vbuf, b, here, vt_s[i, :, r:r + 1])

        @pl.when(i < 2)
        def _():
            w_relay(i + 1)

        @pl.when(i < 3)
        def _():
            w_forward(i)

        return carry

    lax.fori_loop(0, rows // 4, quad, 0)

    w_finish(0)
    h1 = (hid_ref[...].astype(F32) + dot_nt(ctx_s[...].astype(BF16), wall[0])).astype(BF16)
    h1_out[...] = h1
    w_finish(1)
    x = rms(h1.astype(F32), ln2_ref[...])
    qc_out[...] = dot_nt(x, wall[1])
    w_finish(2)
    woc_out[...] = wall[2]
    for copy in heads_of:
        copy.wait()

    for d in range(1, n):
        h_copy(me, lax.rem(me + d, n)).wait_send()
        a_copy(me, lax.rem(me + d, n)).wait_send()
    for t in range(3):
        for dev in (right, left, partner):
            w_copy(t, me, dev).wait_send()
        for src in (right, left, far):
            f_copy(t, src, partner).wait_send()
        l_copy(t, 0, left, right).wait_send()
        l_copy(t, 1, right, left).wait_send()


def cross_kernel(heads, lens_ref, qc_ref, h1_ref, ln3_ref, woc_ref, kbuf, vbuf, khead, vhead, ck_ref, cv_ref,
                 h2_out, x2_out, nk_out, nv_out,
                 ring, scores, probs, qbd, qf_s, ctx_s, item_row, item_col,
                 rsem, kout, vout):
    rows, width = qc_ref.shape
    src_len = ck_ref.shape[2]
    heads_pad = qbd.shape[1]
    head_dim = width // heads
    cap = item_row.shape[0]
    diag = head_mask(heads_pad, width, head_dim)

    total = 0
    for b in range(rows):
        count = (lens_ref[b, 0] - 1) // CHUNK
        for c in range(src_len // CHUNK - 1):
            @pl.when(c < count)
            def _(b=b, c=c, at=total + c):
                item_row[at] = b
                item_col[at] = c + 1

        total = total + count
    groups = (total + GROUP - 1) // GROUP
    padded = groups * GROUP

    def fill(i, carry):
        item_row[i] = rows
        item_col[i] = 0
        return carry

    lax.fori_loop(total, padded, fill, 0)

    def fetch(s):
        slot = lax.rem(s, SLOTS)

        def start(src, i):
            b = jnp.minimum(item_row[i], rows - 1)
            c = pl.multiple_of(item_col[i] * CHUNK, CHUNK)
            pltpu.make_async_copy(src.at[b, :, pl.ds(c, CHUNK)], ring.at[slot], rsem.at[slot]).start()

        @pl.when(s < padded)
        def _():
            start(ck_ref, s)

        @pl.when((s >= padded) & (s < 2 * padded))
        def _():
            start(cv_ref, s - padded)

    def arrive(s):
        slot = lax.rem(s, SLOTS)
        pltpu.make_async_copy(ck_ref.at[0, :, pl.ds(0, CHUNK)], ring.at[slot], rsem.at[slot]).wait()
        return slot

    lax.fori_loop(0, SLOTS, lambda s, c: (fetch(s), c)[1], 0)
    for b in range(rows):
        pltpu.make_async_copy(kbuf.at[b], nk_out.at[b], kout.at[b]).start()

    qf_s[...] = qc_ref[...]
    for b in range(rows):
        qbd[b] = jnp.where(diag, jnp.broadcast_to(qf_s[b:b + 1, :], diag.shape), 0.0).astype(BF16)
    qbd[rows] = jnp.zeros_like(qbd[rows])
    ctx_s[...] = jnp.zeros_like(ctx_s)

    def score_head(i, carry):
        for r in range(GROUP):
            b = i * GROUP + r
            scores[b, :, 0:CHUNK] = dot_nn(qbd[b], khead[b])
        return carry

    lax.fori_loop(0, rows // GROUP, score_head, 0)

    def group_items(base, g):
        slots = [arrive(base + g * GROUP + r) for r in range(GROUP)]
        items = [g * GROUP + r for r in range(GROUP)]
        return [(s, item_row[i], pl.multiple_of(item_col[i] * CHUNK, CHUNK)) for s, i in zip(slots, items)]

    def score_group(g, carry):
        items = group_items(0, g)
        outs = [dot_nn(qbd[b], ring[slot]) for slot, b, c in items]
        for o, (slot, b, c) in zip(outs, items):
            scores[b, :, pl.ds(c, CHUNK)] = o
        for r in range(GROUP):
            fetch(g * GROUP + r + SLOTS)
        return carry

    lax.fori_loop(0, groups, score_group, 0)

    col = lax.broadcasted_iota(jnp.int32, (heads_pad, src_len), 1)

    def soft(i, carry):
        for r in range(4):
            b = i * 4 + r
            s = jnp.where(col < lens_ref[b, 0], scores[b], NEG_BIG)
            probs[b] = softmax_rows(s).astype(BF16)
        return carry

    lax.fori_loop(0, rows // 4, soft, 0)
    probs[rows] = jnp.zeros_like(probs[rows])

    for b in range(rows):
        pltpu.make_async_copy(vbuf.at[b], nv_out.at[b], vout.at[b]).start()

    def fold(full):
        return jnp.sum(jnp.where(diag, full, 0.0), axis=0, keepdims=True)

    def value_head(i, carry):
        outs = [dot_nt(probs[i * GROUP + r, :, 0:CHUNK], vhead[i * GROUP + r]) for r in range(GROUP)]
        for r in range(GROUP):
            ctx_s[pl.ds(i * GROUP + r, 1), :] = fold(outs[r])
        return carry

    lax.fori_loop(0, rows // GROUP, value_head, 0)

    def value_group(g, carry):
        items = group_items(padded, g)
        outs = [dot_nt(probs[b, :, pl.ds(c, CHUNK)], ring[slot]) for slot, b, c in items]
        for o, (slot, b, c) in zip(outs, items):
            ctx_s[pl.ds(b, 1), :] = ctx_s[pl.ds(b, 1), :] + fold(o)
        for r in range(GROUP):
            fetch(padded + g * GROUP + r + SLOTS)
        return carry

    lax.fori_loop(0, groups, value_group, 0)

    h1 = h1_ref[...].astype(F32)
    h2 = (h1 + dot_nt(ctx_s[0:rows, :].astype(BF16), woc_ref[...])).astype(BF16)
    h2_out[...] = h2
    x2_out[...] = rms(h2.astype(F32), ln3_ref[...])
    for b in range(rows):
        pltpu.make_async_copy(kbuf.at[b], nk_out.at[b], kout.at[b]).wait()
        pltpu.make_async_copy(vbuf.at[b], nv_out.at[b], vout.at[b]).wait()


def ffn_kernel(n, x2_ref, h2_ref, idx_ref, router_ref, win_ref, wout_ref, out_ref,
               xall, idx_s, iall, rall, win, wout, act, stage, got,
               isem, osem, xsend, xrecv, jsend, jrecv, rsend, rrecv, ysend, yrecv):
    me = lax.axis_index("ws")
    rows, model = x2_ref.shape
    experts, _, hidden = win_ref.shape
    group = rows * n
    capacity = (2 * group + experts - 1) // experts

    for e in range(experts):
        pltpu.make_async_copy(win_ref.at[e], win.at[e], isem.at[e]).start()
    for e in range(experts):
        pltpu.make_async_copy(wout_ref.at[e], rows_of(wout, e, hidden), osem.at[e]).start()

    eye = (lax.broadcasted_iota(jnp.int32, (rows, rows), 0) == lax.broadcasted_iota(jnp.int32, (rows, rows), 1))
    idx_col = jnp.sum(jnp.where(eye, jnp.broadcast_to(idx_ref[...].astype(F32), (rows, rows)), 0.0),
                      axis=-1, keepdims=True)
    idx_s[...] = jnp.broadcast_to(idx_col, idx_s.shape)
    enter(me, n)

    def x_copy(src, dev):
        return remote(x2_ref, rows_of(xall, src, rows), xsend.at[dev], xrecv.at[src], dev)

    def i_copy(src, dev):
        return remote(idx_s, rows_of(iall, src, rows), jsend.at[dev], jrecv.at[src], dev)

    def r_copy(src, dev):
        return remote(router_ref, rall.at[src], rsend.at[dev], rrecv.at[src], dev)

    for copy in (x_copy, i_copy, r_copy):
        for d in range(1, n):
            copy(me, lax.rem(me + d, n)).start()
    mine = pl.ds(pl.multiple_of(me * rows, rows), rows)
    xall[mine, :] = x2_ref[...]
    iall[mine, :] = idx_s[...]
    rall[me] = router_ref[...]
    for copy in (x_copy, i_copy, r_copy):
        for d in range(1, n):
            copy(lax.rem(me + n - d, n), me).wait_recv()

    x = xall[...]
    chosen = iall[:, 0:1]
    for e in range(experts):
        pltpu.make_async_copy(win_ref.at[e], win.at[e], isem.at[e]).wait()
        u = jnp.maximum(dot_nn(x, win[e]), 0.0)
        act[:, e * hidden:(e + 1) * hidden] = jnp.where(chosen == float(e), u, 0.0).astype(BF16)
    for e in range(experts):
        pltpu.make_async_copy(wout_ref.at[e], rows_of(wout, e, hidden), osem.at[e]).wait()

    halves, _, _, span = stage.shape

    def y_copy(h, src, dev):
        return remote(stage.at[h, dev], got.at[h, src], ysend.at[h, dev], yrecv.at[h, src], dev)

    for h in range(halves):
        y = dot_nn(act[...], wout[:, h * span:(h + 1) * span])
        for j in range(n):
            stage[h, j] = y[j * rows:(j + 1) * rows, :]
        for d in range(1, n):
            y_copy(h, me, lax.rem(me + d, n)).start()
        got[h, me] = stage[h, me]

    xr = x2_ref[...].astype(F32)
    logits = [jnp.sum(xr * rall[e], axis=-1, keepdims=True) for e in range(experts)]
    top = functools.reduce(jnp.maximum, logits)
    exps = [jnp.exp(v - top) for v in logits]
    denom = functools.reduce(jnp.add, exps)
    my_idx = idx_s[:, 0:1]
    gate = functools.reduce(jnp.add, [jnp.where(my_idx == float(e), exps[e] / denom, 0.0) for e in range(experts)])
    others = jnp.transpose(iall[...])[0:rows, :]
    row = me * rows + lax.broadcasted_iota(jnp.int32, (rows, group), 0)
    col = lax.broadcasted_iota(jnp.int32, (rows, group), 1)
    slot = jnp.sum(jnp.where((others == my_idx) & (col < row), 1.0, 0.0), axis=-1, keepdims=True)
    gate = jnp.where(slot < float(capacity), gate, 0.0)

    for h in range(halves):
        for d in range(1, n):
            y_copy(h, lax.rem(me + n - d, n), me).wait_recv()
        y = functools.reduce(jnp.add, [got[h, s] for s in range(n)]).astype(BF16).astype(F32)
        part = slice(h * span, (h + 1) * span)
        out_ref[:, part] = (h2_ref[:, part].astype(F32) + y * gate).astype(BF16)

    for d in range(1, n):
        dev = lax.rem(me + d, n)
        for copy in (x_copy, i_copy, r_copy):
            copy(me, dev).wait_send()
        for h in range(halves):
            y_copy(h, me, dev).wait_send()


def solution(mesh):
    n = mesh.shape['ws']
    row_axes = ('dp', 'ws')
    row_vec = P(row_axes)
    row_mat = P(row_axes, None)
    cache_spec = P(row_axes, None, None, None)
    col_split = P(None, 'ws')
    in_specs = (row_mat, cache_spec, cache_spec, cache_spec, cache_spec, row_vec, row_mat, P(None, None), row_vec,
                P(None), P(None), P(None), col_split, col_split, col_split, col_split, col_split, col_split,
                col_split, P(None, None, 'ws'), P(None, 'ws', None))
    out_specs = (row_mat, cache_spec, cache_spec)
    dma = pltpu.SemaphoreType.DMA

    def decoder_block(hidden, self_k, self_v, cross_k, cross_v, positions, enc_mask, rel_bias, expert_idx,
                      ln_self, ln_cross, ln_ffn, wq_self, wk_self, wv_self, wo_self, wq_cross, wo_cross,
                      w_router, w_in, w_out):
        rows, model = hidden.shape
        _, heads, cache_len, head_dim = self_k.shape
        src_len = cross_k.shape[2]
        width = heads * head_dim
        cols = wq_self.shape[1]
        heads_pad = (heads + 15) // 16 * 16
        experts, _, ff = w_in.shape

        def flat(cache):
            return jnp.swapaxes(cache, 2, 3).reshape(rows, width, cache.shape[2])

        def unflat(cache):
            return jnp.swapaxes(cache.reshape(rows, heads, head_dim, cache.shape[2]), 2, 3)

        sds = jax.ShapeDtypeStruct
        sk, sv, ck, cv = flat(self_k), flat(self_v), flat(cross_k), flat(cross_v)
        def stay(x):
            return pltpu.with_memory_space_constraint(x, pltpu.HBM)

        head_shape = (rows, width, CHUNK)
        qc, h1, lens, woc, ku, vu, kh, vh = pl.pallas_call(
            functools.partial(self_kernel, n, heads),
            name="self_attention",
            out_shape=(sds((rows, width), F32), sds((rows, model), BF16), sds((rows, 128), jnp.int32),
                       pltpu.VMEM((model, width), BF16), pltpu.VMEM(sk.shape, BF16), pltpu.VMEM(sv.shape, BF16),
                       pltpu.VMEM(head_shape, BF16), pltpu.VMEM(head_shape, BF16)),
            in_specs=[smem()] + [vmem()] * 5 + [hbm()] * 10,
            out_specs=tuple([vmem()] * 8),
            scratch_shapes=[
                pltpu.VMEM((rows * n, model), BF16), pltpu.VMEM((n, rows, 384), BF16),
                pltpu.VMEM((n, rows, 384), BF16), pltpu.VMEM((3, cols, model), BF16), pltpu.VMEM((3, width, model), BF16),
                pltpu.VMEM((rows, width), F32), pltpu.VMEM((rows, width), F32), pltpu.VMEM((rows, width), F32),
                pltpu.VMEM((rows // 4, width, 4), F32), pltpu.VMEM((rows // 4, width, 4), F32),
                pltpu.VMEM((rows * heads_pad, width), BF16), pltpu.VMEM((rows * heads_pad, 128), F32),
                pltpu.VMEM((rows, width), F32), pltpu.VMEM((heads_pad, cache_len), F32),
                dma((6,)), dma((rows,)), dma((rows,)), dma((2,)), dma((n,)), dma((n,)), dma((n,)), dma((n,)),
                dma((3, n)), dma((3, n)), dma((3, n)), dma((3, n)), dma((3, 2)), dma((3, 2))],
            compiler_params=pltpu.CompilerParams(collective_id=0, has_side_effects=True,
                                                 vmem_limit_bytes=SELF_VMEM),
        )(*(stay(x) for x in (positions, hidden, enc_mask, rel_bias, ln_self, ln_cross,
                             wq_self.T, wk_self.T, wv_self.T, wo_self.T, wq_cross.T, wo_cross.T, sk, sv, ck, cv)))

        items = rows * (src_len // CHUNK) + GROUP
        h2, x2, nk, nv = pl.pallas_call(
            functools.partial(cross_kernel, heads),
            name="cross_attention",
            out_shape=(sds((rows, model), BF16), sds((rows, model), BF16), sds(sk.shape, BF16), sds(sv.shape, BF16)),
            in_specs=[smem()] + [vmem()] * 8 + [hbm()] * 2,
            out_specs=(vmem(), vmem(), hbm(), hbm()),
            scratch_shapes=[
                pltpu.VMEM((SLOTS, width, CHUNK), BF16), pltpu.VMEM((rows + 1, heads_pad, src_len), F32),
                pltpu.VMEM((rows + 1, heads_pad, src_len), BF16), pltpu.VMEM((rows + 1, heads_pad, width), BF16),
                pltpu.VMEM((rows, width), F32),
                pltpu.VMEM((rows + 8, width), F32), pltpu.SMEM((items,), jnp.int32), pltpu.SMEM((items,), jnp.int32),
                dma((SLOTS,)), dma((rows,)), dma((rows,))],
            compiler_params=pltpu.CompilerParams(vmem_limit_bytes=CROSS_VMEM),
        )(lens, qc, h1, stay(ln_ffn), woc, ku, vu, kh, vh, stay(ck), stay(cv))

        halves = 2
        out = pl.pallas_call(
            functools.partial(ffn_kernel, n),
            name="switch_ffn",
            out_shape=sds((rows, model), BF16),
            in_specs=[vmem()] * 4 + [hbm(), hbm()],
            out_specs=vmem(),
            scratch_shapes=[
                pltpu.VMEM((rows * n, model), BF16), pltpu.VMEM((rows, 128), F32), pltpu.VMEM((rows * n, 128), F32),
                pltpu.VMEM((n, 1, model), F32), pltpu.VMEM(w_in.shape, BF16), pltpu.VMEM((experts * w_out.shape[1], model), BF16),
                pltpu.VMEM((rows * n, experts * ff), BF16), pltpu.VMEM((halves, n, rows, model // halves), F32),
                pltpu.VMEM((halves, n, rows, model // halves), F32),
                dma((experts,)), dma((experts,)), dma((n,)), dma((n,)), dma((n,)), dma((n,)), dma((n,)), dma((n,)),
                dma((halves, n)), dma((halves, n))],
            compiler_params=pltpu.CompilerParams(collective_id=1, has_side_effects=True,
                                                 vmem_limit_bytes=FFN_VMEM),
        )(x2, h2, stay(expert_idx.reshape(1, -1)), stay(w_router.T), stay(w_in), stay(w_out))
        return out, unflat(nk), unflat(nv)

    return jax.shard_map(decoder_block, mesh=mesh, in_specs=in_specs, out_specs=out_specs, check_vma=False)
```

profile of v0, /device:TPU:113, one launch (start us, length us, event | category | flops | bytes accessed | tf_op | source)
XLA Modules:
  0.0 73.3 jit_solution(2814043410816609003)
XLA Ops:
  0.6 34.2 %self_attention.1 = (f32[16,768]{1,0:T(8,128)S(1)}, bf16[16,768]{1,0:T(8,128)(2,1)S(1)}, s32[16,128]{1,0:T(8,128)S(1)}, bf16[768,768]{1,0:T(8,128)(2,1)S(1)}, bf...) custom-call(s32[16]{0:T(128)} %pos_ref.1, ...), custom_call_target="tpu_custom_call" | custom-call | tf_op jit(solution)/shard_map/self_attention/pallas_call | solution.py:535
  34.9 18.0 %cross_attention.1 = (bf16[16,768]{1,0:T(8,128)(2,1)S(1)}, bf16[16,768]{1,0:T(8,128)(2,1)S(1)}, bf16[16,768,384]{2,1,0:T(8,128)(2,1)}, bf16[16,768,384]{2,1,0:T(8,128)(2,1)}) custom-call(s32[16,128]{1,0:T(8,128)S(1)} %get-tuple-element.15.lens_ref, f32[16,768]{1,0:T(8,128)S(1)} %get-tuple-element.16.qc_ref, bf16[16,768]{1,0:T(8,128)(2,1)S(1)} %get-tuple-element.17.h1_ref, ...), custom_call_target="tpu_custom_call" | custom-call | tf_op jit(solution)/shard_map/cross_attention/pallas_call | solution.py:558
  52.9 19.8 %switch_ffn.1 = bf16[16,768]{1,0:T(8,128)(2,1)S(1)} custom-call(bf16[16,768]{1,0:T(8,128)(2,1)S(1)} %get-tuple-element.23.x2_ref, bf16[16,768]{1,0:T(8,128)(2,1)S(1)} %get-tuple-element.24.h2_ref, s32[1,16]{1,0:T(1,128)} %bitcast.39, f32[1,768]{1,0:T(1,128)} %bitcast.38, bf16[8,768,384]{2,1,0:T(8,128)(2,1)} %win_ref.1, bf16[8,384,768]{2,1,0:T(8,128)(2,1)} %wout_ref.1), custom_call_target="tpu_custom_call" | custom-call | tf_op jit(solution)/shard_map/switch_ffn/pallas_call | solution.py:574
  72.7 0.6 copy.25
where the time goes:
time: 73.7 us; the launch traced here: 73.3 us
  Pallas kernels  72.1 us (98%)
    pallas_call x1, Pallas kernels, decoder_block(): pl.pallas_call(functools.partial(self_kernel, n, heads), name='self_atten...  34.2 us
    pallas_call x1, Pallas kernels, decoder_block(): pl.pallas_call(functools.partial(ffn_kernel, n), name='switch_ffn', out_s...  19.8 us
    pallas_call x1, Pallas kernels, decoder_block(): pl.pallas_call(functools.partial(cross_kernel, heads), name='cross_attent...  18 us

commit v1 on v0

--- a/solution.py
+++ b/solution.py
@@ -82,22 +82,20 @@
                 for i, w in enumerate((wo_ref, wqc_ref, woc_ref))]
     for copy in locals_:
         copy.start()
+    heads_of = [pltpu.make_async_copy(src.at[:, :, pl.ds(0, CHUNK)], dst, chsem.at[i])
+                for i, (src, dst) in enumerate(((ck_ref, khead), (cv_ref, vhead)))]
+
+    stage[...] = jnp.zeros_like(stage)
+    enter(me, n)
+
+    def h_copy(src, dev):
+        return remote(hid_ref, rows_of(hall, src, rows), hsend.at[dev], hrecv.at[src], dev)
+
+    for d in range(1, n):
+        h_copy(me, lax.rem(me + d, n)).start()
     for b in range(rows):
         pltpu.make_async_copy(sk_ref.at[b], kbuf.at[b], ksem.at[b]).start()
         pltpu.make_async_copy(sv_ref.at[b], vbuf.at[b], vsem.at[b]).start()
-    heads_of = [pltpu.make_async_copy(src.at[:, :, pl.ds(0, CHUNK)], dst, chsem.at[i])
-                for i, (src, dst) in enumerate(((ck_ref, khead), (cv_ref, vhead)))]
-    for copy in heads_of:
-        copy.start()
-
-    stage[...] = jnp.zeros_like(stage)
-    enter(me, n)
-
-    def h_copy(src, dev):
-        return remote(hid_ref, rows_of(hall, src, rows), hsend.at[dev], hrecv.at[src], dev)
-
-    for d in range(1, n):
-        h_copy(me, lax.rem(me + d, n)).start()
 
     chip, core = me // 2, lax.rem(me, 2)
     def w_copy(t, src, dev):
@@ -170,7 +168,10 @@
     for d in range(1, n):
         a_copy(me, lax.rem(me + d, n)).start()
     got[me] = stage[me]
+    for copy in heads_of:
+        copy.start()
     w_start(1)
+    w_relay(0)
     w_start(2)
     for d in range(1, n):
         a_copy(lax.rem(me + n - d, n), me).wait_recv()
@@ -213,8 +214,6 @@
             old = buf[b, :, part].reshape(width // 16, 16, 128)
             buf[b, :, part] = jnp.where(here[None, :, part], wide, old).reshape(width, 128)
 
-    w_relay(0)
-
     def quad(i, carry):
         rows4 = [i * 4 + r for r in range(4)]
         head_rows = [pl.ds(pl.multiple_of(b * heads_pad, heads_pad), heads_pad) for b in rows4]
@@ -239,21 +238,23 @@
             insert(kbuf, b, here, kt_s[i, :, r:r + 1])
             insert(vbuf, b, here, vt_s[i, :, r:r + 1])
 
-        @pl.when(i < 2)
+        @pl.when(i == 0)
         def _():
-            w_relay(i + 1)
-
-        @pl.when(i < 3)
+            w_forward(0)
+
+        @pl.when((i == 1) | (i == 2))
         def _():
-            w_forward(i)
+            w_relay(i)
 
         return carry
 
     lax.fori_loop(0, rows // 4, quad, 0)
 
+    w_forward(1)
     w_finish(0)
     h1 = (hid_ref[...].astype(F32) + dot_nt(ctx_s[...].astype(BF16), wall[0])).astype(BF16)
     h1_out[...] = h1
+    w_forward(2)
     w_finish(1)
     x = rms(h1.astype(F32), ln2_ref[...])
     qc_out[...] = dot_nt(x, wall[1])
@@ -407,19 +408,14 @@
 
 
 def ffn_kernel(n, x2_ref, h2_ref, idx_ref, router_ref, win_ref, wout_ref, out_ref,
-               xall, idx_s, iall, rall, win, wout, act, stage, got,
-               isem, osem, xsend, xrecv, jsend, jrecv, rsend, rrecv, ysend, yrecv):
+               xall, idx_s, iall, rall, win, wout, act, stage, pair, total, got,
+               isem, osem, xsend, xrecv, jsend, jrecv, rsend, rrecv, psend, precv, ysend, yrecv):
     me = lax.axis_index("ws")
     rows, model = x2_ref.shape
     experts, _, hidden = win_ref.shape
     group = rows * n
     capacity = (2 * group + experts - 1) // experts
 
-    for e in range(experts):
-        pltpu.make_async_copy(win_ref.at[e], win.at[e], isem.at[e]).start()
-    for e in range(experts):
-        pltpu.make_async_copy(wout_ref.at[e], rows_of(wout, e, hidden), osem.at[e]).start()
-
     eye = (lax.broadcasted_iota(jnp.int32, (rows, rows), 0) == lax.broadcasted_iota(jnp.int32, (rows, rows), 1))
     idx_col = jnp.sum(jnp.where(eye, jnp.broadcast_to(idx_ref[...].astype(F32), (rows, rows)), 0.0),
                       axis=-1, keepdims=True)
@@ -438,6 +434,10 @@
     for copy in (x_copy, i_copy, r_copy):
         for d in range(1, n):
             copy(me, lax.rem(me + d, n)).start()
+    for e in range(experts):
+        pltpu.make_async_copy(win_ref.at[e], win.at[e], isem.at[e]).start()
+    for e in range(experts):
+        pltpu.make_async_copy(wout_ref.at[e], rows_of(wout, e, hidden), osem.at[e]).start()
     mine = pl.ds(pl.multiple_of(me * rows, rows), rows)
     xall[mine, :] = x2_ref[...]
     iall[mine, :] = idx_s[...]
@@ -455,18 +455,31 @@
     for e in range(experts):
         pltpu.make_async_copy(wout_ref.at[e], rows_of(wout, e, hidden), osem.at[e]).wait()
 
-    halves, _, _, span = stage.shape
-
-    def y_copy(h, src, dev):
-        return remote(stage.at[h, dev], got.at[h, src], ysend.at[h, dev], yrecv.at[h, src], dev)
+    halves, _, chips, _, span = stage.shape
+    chip, core = me // 2, lax.rem(me, 2)
+    partner = me + 1 - 2 * core
+
+    def p_copy(h):
+        return remote(stage.at[h, 1 - core], pair.at[h], psend.at[h], precv.at[h], partner)
+
+    def y_copy(h, src, dst):
+        return remote(total.at[h, dst], got.at[h, src], ysend.at[h, dst], yrecv.at[h, src], dst * 2 + core)
+
+    def send_sums(h):
+        p_copy(h).wait_recv()
+        total[h] = stage[h, core] + pair[h]
+        for d in range(1, chips):
+            y_copy(h, chip, lax.rem(chip + d, chips)).start()
+        got[h, chip] = total[h, chip]
 
     for h in range(halves):
         y = dot_nn(act[...], wout[:, h * span:(h + 1) * span])
         for j in range(n):
-            stage[h, j] = y[j * rows:(j + 1) * rows, :]
-        for d in range(1, n):
-            y_copy(h, me, lax.rem(me + d, n)).start()
-        got[h, me] = stage[h, me]
+            stage[h, j % 2, j // 2] = y[j * rows:(j + 1) * rows, :]
+        p_copy(h).start()
+        if h:
+            send_sums(h - 1)
+    send_sums(halves - 1)
 
     xr = x2_ref[...].astype(F32)
     logits = [jnp.sum(xr * rall[e], axis=-1, keepdims=True) for e in range(experts)]
@@ -482,9 +495,9 @@
     gate = jnp.where(slot < float(capacity), gate, 0.0)
 
     for h in range(halves):
-        for d in range(1, n):
-            y_copy(h, lax.rem(me + n - d, n), me).wait_recv()
-        y = functools.reduce(jnp.add, [got[h, s] for s in range(n)]).astype(BF16).astype(F32)
+        for d in range(1, chips):
+            y_copy(h, lax.rem(chip + d, chips), chip).wait_recv()
+        y = functools.reduce(jnp.add, [got[h, s] for s in range(chips)]).astype(BF16).astype(F32)
         part = slice(h * span, (h + 1) * span)
         out_ref[:, part] = (h2_ref[:, part].astype(F32) + y * gate).astype(BF16)
 
@@ -492,8 +505,10 @@
         dev = lax.rem(me + d, n)
         for copy in (x_copy, i_copy, r_copy):
             copy(me, dev).wait_send()
-        for h in range(halves):
-            y_copy(h, me, dev).wait_send()
+    for h in range(halves):
+        p_copy(h).wait_send()
+        for d in range(1, chips):
+            y_copy(h, chip, lax.rem(chip + d, chips)).wait_send()
 
 
 def solution(mesh):
@@ -570,7 +585,7 @@
             compiler_params=pltpu.CompilerParams(vmem_limit_bytes=CROSS_VMEM),
         )(lens, qc, h1, stay(ln_ffn), woc, ku, vu, kh, vh, stay(ck), stay(cv))
 
-        halves = 2
+        halves = 3
         out = pl.pallas_call(
             functools.partial(ffn_kernel, n),
             name="switch_ffn",
@@ -580,10 +595,11 @@
             scratch_shapes=[
                 pltpu.VMEM((rows * n, model), BF16), pltpu.VMEM((rows, 128), F32), pltpu.VMEM((rows * n, 128), F32),
                 pltpu.VMEM((n, 1, model), F32), pltpu.VMEM(w_in.shape, BF16), pltpu.VMEM((experts * w_out.shape[1], model), BF16),
-                pltpu.VMEM((rows * n, experts * ff), BF16), pltpu.VMEM((halves, n, rows, model // halves), F32),
-                pltpu.VMEM((halves, n, rows, model // halves), F32),
+                pltpu.VMEM((rows * n, experts * ff), BF16), pltpu.VMEM((halves, 2, n // 2, rows, model // halves), F32),
+                pltpu.VMEM((halves, n // 2, rows, model // halves), F32), pltpu.VMEM((halves, n // 2, rows, model // halves), F32),
+                pltpu.VMEM((halves, n // 2, rows, model // halves), F32),
                 dma((experts,)), dma((experts,)), dma((n,)), dma((n,)), dma((n,)), dma((n,)), dma((n,)), dma((n,)),
-                dma((halves, n)), dma((halves, n))],
+                dma((halves,)), dma((halves,)), dma((halves, n // 2)), dma((halves, n // 2))],
             compiler_params=pltpu.CompilerParams(collective_id=1, has_side_effects=True,
                                                  vmem_limit_bytes=FFN_VMEM),
         )(x2, h2, stay(expert_idx.reshape(1, -1)), stay(w_router.T), stay(w_in), stay(w_out))

time: 73.7 us -> 66.4 us (0.901)
  Pallas kernels: 72.1 us -> 64.1 us
    pallas_call x1, Pallas kernels: 34.2 us -> 29.1 us  [decoder_block(): pl.pallas_call(functools.partial(self_kernel, n, heads), name='self_atten...]
    pallas_call x1, Pallas kernels: 18 us -> 16 us  [decoder_block(): pl.pallas_call(functools.partial(cross_kernel, heads), name='cross_attent...]
    pallas_call x1, Pallas kernels: 19.8 us -> 19 us  [decoder_block(): pl.pallas_call(functools.partial(ffn_kernel, n), name='switch_ffn', out_s...]
where the time goes in v1:
time: 66.4 us; the launch traced here: 65.4 us
  Pallas kernels  64.1 us (97%)
    pallas_call x1, Pallas kernels, decoder_block(): pl.pallas_call(functools.partial(self_kernel, n, heads), name='self_atten...  29.1 us
    pallas_call x1, Pallas kernels, decoder_block(): pl.pallas_call(functools.partial(ffn_kernel, n), name='switch_ffn', out_s...  19 us
    pallas_call x1, Pallas kernels, decoder_block(): pl.pallas_call(functools.partial(cross_kernel, heads), name='cross_attent...  16 us

profile of v1, /device:TPU:113, one launch (start us, length us, event | category | flops | bytes accessed | tf_op | source)
XLA Modules:
  0.0 65.4 jit_solution(14842617815314363128)
XLA Ops:
  0.6 29.1 %self_attention.1 = (f32[16,768]{1,0:T(8,128)S(1)}, bf16[16,768]{1,0:T(8,128)(2,1)S(1)}, s32[16,128]{1,0:T(8,128)S(1)}, bf16[768,768]{1,0:T(8,128)(2,1)S(1)}, bf...) custom-call(s32[16]{0:T(128)} %pos_ref.1, ...), custom_call_target="tpu_custom_call" | custom-call | tf_op jit(solution)/shard_map/self_attention/pallas_call | solution.py:550
  29.7 16.0 %cross_attention.1 = (bf16[16,768]{1,0:T(8,128)(2,1)S(1)}, bf16[16,768]{1,0:T(8,128)(2,1)S(1)}, bf16[16,768,384]{2,1,0:T(8,128)(2,1)}, bf16[16,768,384]{2,1,0:T(8,128)(2,1)}) custom-call(s32[16,128]{1,0:T(8,128)S(1)} %get-tuple-element.15.lens_ref, f32[16,768]{1,0:T(8,128)S(1)} %get-tuple-element.16.qc_ref, bf16[16,768]{1,0:T(8,128)(2,1)S(1)} %get-tuple-element.17.h1_ref, ...), custom_call_target="tpu_custom_call" | custom-call | tf_op jit(solution)/shard_map/cross_attention/pallas_call | solution.py:573
  45.7 19.0 %switch_ffn.1 = bf16[16,768]{1,0:T(8,128)(2,1)S(1)} custom-call(bf16[16,768]{1,0:T(8,128)(2,1)S(1)} %get-tuple-element.23.x2_ref, bf16[16,768]{1,0:T(8,128)(2,1)S(1)} %get-tuple-element.24.h2_ref, s32[1,16]{1,0:T(1,128)} %bitcast.39, f32[1,768]{1,0:T(1,128)} %bitcast.38, bf16[8,768,384]{2,1,0:T(8,128)(2,1)} %win_ref.1, bf16[8,384,768]{2,1,0:T(8,128)(2,1)} %wout_ref.1), custom_call_target="tpu_custom_call" | custom-call | tf_op jit(solution)/shard_map/switch_ffn/pallas_call | solution.py:589
  64.8 0.6 copy.25

commit v2 on v1

--- a/solution.py
+++ b/solution.py
@@ -13,9 +13,9 @@
 BF16 = jnp.bfloat16
 CHUNK = 256
 GROUP = 4
-SLOTS = 24
+SLOTS = 32
 SELF_VMEM = 16 * 1024 * 1024
-CROSS_VMEM = 18 * 1024 * 1024
+CROSS_VMEM = 21 * 1024 * 1024
 FFN_VMEM = 20 * 1024 * 1024
 
 vmem = functools.partial(pl.BlockSpec, memory_space=pltpu.VMEM)
@@ -39,6 +39,10 @@
 def remote(src, dst, send, recv, dev):
     return pltpu.make_async_remote_copy(src_ref=src, dst_ref=dst, send_sem=send, recv_sem=recv,
                                         device_id={"ws": dev}, device_id_type=MESH)
+
+
+def far_first(n):
+    return sorted(range(1, n), key=lambda d: abs(d - n // 2))
 
 
 def enter(me, n):
@@ -50,6 +54,40 @@
 
 def rows_of(ref, i, rows):
     return ref.at[pl.ds(pl.multiple_of(i * rows, rows), rows)]
+
+
+def group_gather(me, n, rows, own, buf, send, recv):
+    core = lax.rem(me, 2)
+    flip = 1 - 2 * core
+    partner = me + flip
+    peers = [lax.rem(me + 2 * d, n) for d in range(1, n // 2)]
+
+    def direct(dev, src):
+        return remote(own, rows_of(buf, src, rows), send.at[dev], recv.at[src], dev)
+
+    def passed(src):
+        piece = rows_of(buf, src, rows)
+        return remote(piece, piece, send.at[src + flip], recv.at[src], partner)
+
+    def start():
+        for dev in (*peers, partner):
+            direct(dev, me).start()
+
+    def finish():
+        for src in peers:
+            direct(me, src).wait_recv()
+            passed(src).start()
+        direct(me, partner).wait_recv()
+        for src in peers:
+            passed(src + flip).wait_recv()
+
+    def drain():
+        for dev in (*peers, partner):
+            direct(dev, me).wait_send()
+        for src in peers:
+            passed(src).wait_send()
+
+    return start, finish, drain
 
 
 def head_mask(heads_pad, width, head_dim):
@@ -88,11 +126,8 @@
     stage[...] = jnp.zeros_like(stage)
     enter(me, n)
 
-    def h_copy(src, dev):
-        return remote(hid_ref, rows_of(hall, src, rows), hsend.at[dev], hrecv.at[src], dev)
-
-    for d in range(1, n):
-        h_copy(me, lax.rem(me + d, n)).start()
+    h_start, h_finish, h_drain = group_gather(me, n, rows, hid_ref, hall, hsend, hrecv)
+    h_start()
     for b in range(rows):
         pltpu.make_async_copy(sk_ref.at[b], kbuf.at[b], ksem.at[b]).start()
         pltpu.make_async_copy(sv_ref.at[b], vbuf.at[b], vsem.at[b]).start()
@@ -154,8 +189,7 @@
     lens_out[...] = jnp.broadcast_to(
         jnp.sum(mask_ref[...].astype(F32), axis=-1, keepdims=True), lens_out.shape).astype(jnp.int32)
 
-    for d in range(1, n):
-        h_copy(lax.rem(me + n - d, n), me).wait_recv()
+    h_finish()
     x = rms(hall[...].astype(F32), ln1_ref[...])
     for i in range(3):
         y = dot_nt(x, wqkv[i]).astype(BF16)
@@ -165,7 +199,7 @@
     def a_copy(src, dev):
         return remote(stage.at[dev], got.at[src], asend.at[dev], arecv.at[src], dev)
 
-    for d in range(1, n):
+    for d in far_first(n):
         a_copy(me, lax.rem(me + d, n)).start()
     got[me] = stage[me]
     for copy in heads_of:
@@ -240,11 +274,15 @@
 
         @pl.when(i == 0)
         def _():
+            w_relay(1)
+
+        @pl.when(i == 1)
+        def _():
             w_forward(0)
 
-        @pl.when((i == 1) | (i == 2))
+        @pl.when(i == 2)
         def _():
-            w_relay(i)
+            w_relay(2)
 
         return carry
 
@@ -264,8 +302,8 @@
         copy.wait()
 
     for d in range(1, n):
-        h_copy(me, lax.rem(me + d, n)).wait_send()
         a_copy(me, lax.rem(me + d, n)).wait_send()
+    h_drain()
     for t in range(3):
         for dev in (right, left, partner):
             w_copy(t, me, dev).wait_send()
@@ -419,7 +457,7 @@
     eye = (lax.broadcasted_iota(jnp.int32, (rows, rows), 0) == lax.broadcasted_iota(jnp.int32, (rows, rows), 1))
     idx_col = jnp.sum(jnp.where(eye, jnp.broadcast_to(idx_ref[...].astype(F32), (rows, rows)), 0.0),
                       axis=-1, keepdims=True)
-    idx_s[...] = jnp.broadcast_to(idx_col, idx_s.shape)
+    idx_s[...] = jnp.broadcast_to(idx_col, idx_s.shape).astype(BF16)
     enter(me, n)
 
     def x_copy(src, dev):
@@ -432,7 +470,7 @@
         return remote(router_ref, rall.at[src], rsend.at[dev], rrecv.at[src], dev)
 
     for copy in (x_copy, i_copy, r_copy):
-        for d in range(1, n):
+        for d in far_first(n):
             copy(me, lax.rem(me + d, n)).start()
     for e in range(experts):
         pltpu.make_async_copy(win_ref.at[e], win.at[e], isem.at[e]).start()
@@ -442,12 +480,12 @@
     xall[mine, :] = x2_ref[...]
     iall[mine, :] = idx_s[...]
     rall[me] = router_ref[...]
-    for copy in (x_copy, i_copy, r_copy):
+    for copy in (x_copy, i_copy):
         for d in range(1, n):
             copy(lax.rem(me + n - d, n), me).wait_recv()
 
     x = xall[...]
-    chosen = iall[:, 0:1]
+    chosen = iall[...].astype(F32)[:, 0:1]
     for e in range(experts):
         pltpu.make_async_copy(win_ref.at[e], win.at[e], isem.at[e]).wait()
         u = jnp.maximum(dot_nn(x, win[e]), 0.0)
@@ -481,14 +519,16 @@
             send_sums(h - 1)
     send_sums(halves - 1)
 
+    for d in range(1, n):
+        r_copy(lax.rem(me + n - d, n), me).wait_recv()
     xr = x2_ref[...].astype(F32)
     logits = [jnp.sum(xr * rall[e], axis=-1, keepdims=True) for e in range(experts)]
     top = functools.reduce(jnp.maximum, logits)
     exps = [jnp.exp(v - top) for v in logits]
     denom = functools.reduce(jnp.add, exps)
-    my_idx = idx_s[:, 0:1]
+    my_idx = idx_s[...].astype(F32)[:, 0:1]
     gate = functools.reduce(jnp.add, [jnp.where(my_idx == float(e), exps[e] / denom, 0.0) for e in range(experts)])
-    others = jnp.transpose(iall[...])[0:rows, :]
+    others = jnp.transpose(iall[...].astype(F32))[0:rows, :]
     row = me * rows + lax.broadcasted_iota(jnp.int32, (rows, group), 0)
     col = lax.broadcasted_iota(jnp.int32, (rows, group), 1)
     slot = jnp.sum(jnp.where((others == my_idx) & (col < row), 1.0, 0.0), axis=-1, keepdims=True)
@@ -593,7 +633,7 @@
             in_specs=[vmem()] * 4 + [hbm(), hbm()],
             out_specs=vmem(),
             scratch_shapes=[
-                pltpu.VMEM((rows * n, model), BF16), pltpu.VMEM((rows, 128), F32), pltpu.VMEM((rows * n, 128), F32),
+                pltpu.VMEM((rows * n, model), BF16), pltpu.VMEM((rows, 128), BF16), pltpu.VMEM((rows * n, 128), BF16),
                 pltpu.VMEM((n, 1, model), F32), pltpu.VMEM(w_in.shape, BF16), pltpu.VMEM((experts * w_out.shape[1], model), BF16),
                 pltpu.VMEM((rows * n, experts * ff), BF16), pltpu.VMEM((halves, 2, n // 2, rows, model // halves), F32),
                 pltpu.VMEM((halves, n // 2, rows, model // halves), F32), pltpu.VMEM((halves, n // 2, rows, model // halves), F32),

time: 66.4 us -> 65.4 us (0.985)
  Pallas kernels: 64.1 us -> 63 us
    pallas_call x1, Pallas kernels: 19 us -> 17.8 us  [decoder_block(): pl.pallas_call(functools.partial(ffn_kernel, n), name='switch_ffn', out_s...]
    pallas_call x1, Pallas kernels: 16 us -> 16.9 us  [decoder_block(): pl.pallas_call(functools.partial(cross_kernel, heads), name='cross_attent...]
    pallas_call x1, Pallas kernels: 29.1 us -> 28.3 us  [decoder_block(): pl.pallas_call(functools.partial(self_kernel, n, heads), name='self_atten...]
where the time goes in v2:
time: 65.4 us; the launch traced here: 64.3 us
  Pallas kernels  63 us (96%)
  between operations  0.66 us (1%)
    pallas_call x1, Pallas kernels, decoder_block(): pl.pallas_call(functools.partial(self_kernel, n, heads), name='self_atten...  28.3 us
    pallas_call x1, Pallas kernels, decoder_block(): pl.pallas_call(functools.partial(ffn_kernel, n), name='switch_ffn', out_s...  17.8 us
    pallas_call x1, Pallas kernels, decoder_block(): pl.pallas_call(functools.partial(cross_kernel, heads), name='cross_attent...  16.9 us

profile of v2, /device:TPU:113, one launch (start us, length us, event | category | flops | bytes accessed | tf_op | source)
XLA Modules:
  0.0 64.3 jit_solution(11439461423291113497)
XLA Ops:
  0.6 28.3 %self_attention.1 = (f32[16,768]{1,0:T(8,128)S(1)}, bf16[16,768]{1,0:T(8,128)(2,1)S(1)}, s32[16,128]{1,0:T(8,128)S(1)}, bf16[768,768]{1,0:T(8,128)(2,1)S(1)}, bf...) custom-call(s32[16]{0:T(128)} %pos_ref.1, ...), custom_call_target="tpu_custom_call" | custom-call | tf_op jit(solution)/shard_map/self_attention/pallas_call | solution.py:590
  28.9 16.9 %cross_attention.1 = (bf16[16,768]{1,0:T(8,128)(2,1)S(1)}, bf16[16,768]{1,0:T(8,128)(2,1)S(1)}, bf16[16,768,384]{2,1,0:T(8,128)(2,1)}, bf16[16,768,384]{2,1,0:T(8,128)(2,1)}) custom-call(s32[16,128]{1,0:T(8,128)S(1)} %get-tuple-element.15.lens_ref, f32[16,768]{1,0:T(8,128)S(1)} %get-tuple-element.16.qc_ref, bf16[16,768]{1,0:T(8,128)(2,1)S(1)} %get-tuple-element.17.h1_ref, ...), custom_call_target="tpu_custom_call" | custom-call | tf_op jit(solution)/shard_map/cross_attention/pallas_call | solution.py:613
  45.9 17.8 %switch_ffn.1 = bf16[16,768]{1,0:T(8,128)(2,1)S(1)} custom-call(bf16[16,768]{1,0:T(8,128)(2,1)S(1)} %get-tuple-element.23.x2_ref, bf16[16,768]{1,0:T(8,128)(2,1)S(1)} %get-tuple-element.24.h2_ref, s32[1,16]{1,0:T(1,128)} %bitcast.39, f32[1,768]{1,0:T(1,128)} %bitcast.38, bf16[8,768,384]{2,1,0:T(8,128)(2,1)} %win_ref.1, bf16[8,384,768]{2,1,0:T(8,128)(2,1)} %wout_ref.1), custom_call_target="tpu_custom_call" | custom-call | tf_op jit(solution)/shard_map/switch_ffn/pallas_call | solution.py:629
  63.7 0.6 copy.25
